TPU v7x, 32 devices: a whole 2x2x4 slice. The times are simulated.
32 devices in a mesh: row: 4 (over x, core), col: 8 (over z, y).
Axes of the slice: x: 2, y: 2, z: 4, core: 2. Of those that a mesh axis runs over, the one named last changes fastest.
Arguments:
- tiles: int32 [4, 8, 8, 128, 128], P('row', 'col'), may hold values from 0 to 1073741823, as said below
- slots: int32 [4, 8, 8], P('row', 'col'), may hold values from 0 to 31, as said below
- factor: float32 [4096, 256], P(('row', 'col')), may hold values from -0.5 to 0.5
- dual: float32 [4096, 256], P(('row', 'col')), may hold values from -0.5 to 0.5
Outputs:
- final_factor: float32 [4096, 256], P(('row', 'col'))
- final_dual: float32 [4096, 256], P(('row', 'col'))
- objective: float32 [3], replicated
- residual: float32 [3], replicated
Inputs may be any that keep to these rules, and one draw needn't show every extreme that they name: `slots`: for every device, 8 distinct block numbers in ascending order. The stored blocks of all devices form a symmetric pattern: the block of rows piece p and columns piece q is stored if and only if the block of rows piece q and columns piece p is; every diagonal block is stored. `tiles`: the stored block of rows piece p and columns piece q is the transpose of the one of rows piece q and columns piece p; diagonal blocks are symmetric.
All inputs are finite; a program needn't handle non-finite values.
Results may differ from a plain program's by a relative error of at most 0.005.
Values may be sent and summed in bfloat16 or wider, within the bound.
A program may use at most 64 MiB of HBM per device.

v0:
```python
import math
import jax
import jax.numpy as jnp
from jax import lax
from jax.sharding import PartitionSpec as P

ITERS = 3
penalty = 2.0
step_size = 0.25
ridge_shift = 0.1
offset = 536870912


def block_weights(integers, vertices):
    unit_scale = math.sqrt(6.0 / vertices) / 2.0**29
    return ((integers - offset).astype(jnp.float32) * unit_scale).astype(jnp.bfloat16)


def unit_rows(values):
    return values * lax.rsqrt(jnp.sum(values * values, axis=1, keepdims=True) + 1e-06)


def local(tiles, slots, factor, dual):
    row_count = lax.axis_size("row")
    col_count = lax.axis_size("col")
    piece_rows = factor.shape[0]
    columns = factor.shape[1]
    vertices = piece_rows * row_count * col_count
    weights = block_weights(tiles.reshape(tiles.shape[2], piece_rows, piece_rows), vertices)
    stored = slots.reshape(-1)
    block_row = stored // row_count
    block_col = stored % row_count

    def combine(partial_value):
        return lax.psum_scatter(partial_value, "col", scatter_dimension=0, tiled=True)

    selector = (block_row[None, :] == jnp.arange(col_count, dtype=jnp.int32)[:, None]).astype(
        jnp.float32
    )
    block_sums = jnp.sum(weights, axis=2, dtype=jnp.float32)
    edge_sums = jnp.dot(selector, block_sums, precision=lax.Precision.HIGHEST)
    degree = combine(edge_sums.reshape(-1))
    current = factor
    lagrange = dual
    projected = unit_rows(current + lagrange / penalty)
    tallies = []
    for iteration in range(ITERS):
        packed = current.astype(jnp.bfloat16)
        own_gram = lax.dot_general(
            packed, packed, (((0,), (0,)), ((), ())), preferred_element_type=jnp.float32
        )
        gram_total = lax.psum(own_gram, ("row", "col"))
        gathered = lax.all_gather(packed, "row", axis=0, tiled=True).reshape(
            -1, piece_rows, columns
        )
        chosen = gathered[block_col]
        products = jnp.einsum("tij,tjk->tik", weights, chosen, preferred_element_type=jnp.float32)
        partial_value = jnp.einsum(
            "at,tik->aik", selector, products, precision=lax.Precision.HIGHEST
        )
        coupled = combine(partial_value.reshape(col_count * piece_rows, columns))
        widened = packed.astype(jnp.float32)
        gradient = degree[:, None] * widened - coupled
        precond = columns / vertices * gram_total + ridge_shift * jnp.eye(
            columns, dtype=jnp.float32
        )
        triangle = jnp.linalg.cholesky(precond)
        descent = 2.0 * gradient - lagrange - penalty * (current - projected)
        current = current + step_size * jax.scipy.linalg.cho_solve((triangle, True), descent.T).T
        projected = unit_rows(current + lagrange / penalty)
        lagrange = lagrange + penalty * (current - projected)
        mismatch = current - projected
        local_sums = jnp.stack([jnp.sum(widened * gradient), jnp.sum(mismatch * mismatch)])
        tallies.append(local_sums)
    stacked = jnp.stack(tallies)
    stacked = lax.psum(stacked, ("row", "col"))
    objective = stacked[:, 0] / (4.0 * vertices)
    residual = stacked[:, 1] / vertices
    return (current, lagrange, objective, residual)


def solution(mesh):
    in_specs = (
        P("row", "col", None, None, None),
        P("row", "col", None),
        P(("row", "col"), None),
        P(("row", "col"), None),
    )
    out_specs = (P(("row", "col"), None), P(("row", "col"), None), P(), P())
    return jax.shard_map(local, mesh=mesh, in_specs=in_specs, out_specs=out_specs, check_vma=False)
```

profile of v0, /device:TPU:0, one launch (start us, length us, event | category | flops | bytes accessed | tf_op | source)
XLA Modules:
  0.0 669.2 jit_solution(12461409791366380685)
XLA Ops:
  8.1 1.0 copy.58
  9.2 0.9 fusion.70
  10.2 7.2 %all_gather.9 = bf16[512,256]{0,1:T(8,128)(2,1)S(1)} all-gather(bf16[128,256]{0,1:T(8,128)(2,1)S(1)} %get-tuple-element.92), channel_id=1, replica_groups=mesh['row'=4,'col'=8] {'row'}, dimensions={0}, use_global_device_ids=true | all-gather | bytes 327680 | tf_op jit(solution)/shard_map/all_gather | solution.py:53
  18.8 1.2 fusion
  20.3 1.3 copy.53
  21.8 22.3 %all-reduce.1 = f32[1024]{0:T(1024)S(1)} all-reduce(f32[1024]{0:T(1024)S(1)} %convolution_bitcast_fusion), channel_id=2, replica_groups=mesh['row'=4,'col'=8] {'col'}, use_global_device_ids=true, to_apply=%region_6.8.clone | all-reduce | flops 1024 | bytes 8192
  46.1 99.0 %all-reduce.6.cloned.1.call-done = f32[256,256]{0,1:T(8,128)} async-done(((f32[256,256]{0,1:T(8,128)}), f32[256,256]{0,1:T(8,128)}) %all-reduce.6.cloned.1.call-update) | async-done | bytes 262160 | tf_op jit(solution)/shard_map/psum | solution.py:52
  145.1 1.0 select_add_fusion.2
  146.2 0.8 copy-done
  147.1 11.7 %cholesky.172 = f32[128,128]{1,0:T(8,128)S(1)} custom-call(f32[128,128]{1,0:T(8,128)S(1)} %cholesky.270), custom_call_target="Cholesky" | custom-call | tf_op jit(solution)/shard_map/jit(cholesky)/cholesky | solution.py:67
  158.9 9.8 %custom-call.17 = f32[1,128,128]{1,2,0:T(8,128)S(1)} custom-call(f32[1,128,128]{2,1,0:T(8,128)S(1)} %get-tuple-element.104), custom_call_target="InvertDiagBlocksLowerTriangular" | custom-call | tf_op jit(solution)/shard_map/jit(cholesky)/cholesky | solution.py:67
  169.2 11.7 %cholesky.189 = f32[128,128]{1,0:T(8,128)S(1)} custom-call(f32[128,128]{1,0:T(8,128)S(1)} %convolution_subtract_fusion.8), custom_call_target="Cholesky" | custom-call | tf_op jit(solution)/shard_map/jit(cholesky)/cholesky | solution.py:67
  183.0 4.2 while.6
  183.8 1.4 bitcast_dynamic-update-slice_fusion.6
  185.8 1.4 bitcast_dynamic-update-slice_fusion.6
  187.2 19.7 %custom-call.18 = f32[2,128,128]{1,2,0:T(8,128)S(1)} custom-call(f32[2,128,128]{2,1,0:T(8,128)S(1)} %get-tuple-element.26), custom_call_target="InvertDiagBlocksLowerTriangular" | custom-call | tf_op jit(solution)/shard_map/jit(_cho_solve)/triangular_solve | solution.py:69
  206.9 1.0 subtract_bitcast_fusion.2
  209.4 5.8 all_gather.10
  215.2 0.9 fusion.72
  218.2 1.2 copy.91
  220.1 126.6 %all-reduce.8.cloned.1.call-done = f32[256,256]{0,1:T(8,128)} async-done(((f32[256,256]{0,1:T(8,128)}), f32[256,256]{0,1:T(8,128)}) %all-reduce.8.cloned.1.call-update) | async-done | bytes 262160 | tf_op jit(solution)/shard_map/psum | solution.py:52
  346.7 1.0 select_add_fusion.1
  347.8 0.8 copy-done.1
  348.7 11.7 %cholesky.206 = f32[128,128]{1,0:T(8,128)S(1)} custom-call(f32[128,128]{1,0:T(8,128)S(1)} %cholesky.273), custom_call_target="Cholesky" | custom-call | tf_op jit(solution)/shard_map/jit(cholesky)/cholesky | solution.py:67
  360.4 9.8 %custom-call.19 = f32[1,128,128]{1,2,0:T(8,128)S(1)} custom-call(f32[1,128,128]{2,1,0:T(8,128)S(1)} %get-tuple-element.100), custom_call_target="InvertDiagBlocksLowerTriangular" | custom-call | tf_op jit(solution)/shard_map/jit(cholesky)/cholesky | solution.py:67
  370.7 11.7 %cholesky.223 = f32[128,128]{1,0:T(8,128)S(1)} custom-call(f32[128,128]{1,0:T(8,128)S(1)} %convolution_subtract_fusion.5), custom_call_target="Cholesky" | custom-call | tf_op jit(solution)/shard_map/jit(cholesky)/cholesky | solution.py:67
  385.1 4.2 while.7
  385.9 1.4 bitcast_dynamic-update-slice_fusion.7
  387.9 1.4 bitcast_dynamic-update-slice_fusion.7
  389.3 19.7 %custom-call.20 = f32[2,128,128]{1,2,0:T(8,128)S(1)} custom-call(f32[2,128,128]{2,1,0:T(8,128)S(1)} %get-tuple-element.27), custom_call_target="InvertDiagBlocksLowerTriangular" | custom-call | tf_op jit(solution)/shard_map/jit(_cho_solve)/triangular_solve | solution.py:69
  409.1 1.6 subtract_bitcast_fusion.1
  412.2 0.9 fusion.68
  413.1 5.8 all_gather.11
  420.9 1.2 copy.90
  422.7 126.8 %all-reduce.10.cloned.1.call-done = f32[256,256]{0,1:T(8,128)} async-done(((f32[256,256]{0,1:T(8,128)}), f32[256,256]{0,1:T(8,128)}) %all-reduce.10.cloned.1.call-update) | async-done | bytes 262160 | tf_op jit(solution)/shard_map/psum | solution.py:52
  549.5 1.0 select_add_fusion
  551.5 11.7 %cholesky.240 = f32[128,128]{1,0:T(8,128)S(1)} custom-call(f32[128,128]{1,0:T(8,128)S(1)} %cholesky.276), custom_call_target="Cholesky" | custom-call | tf_op jit(solution)/shard_map/jit(cholesky)/cholesky | solution.py:67
  563.3 9.8 %custom-call.21 = f32[1,128,128]{1,2,0:T(8,128)S(1)} custom-call(f32[1,128,128]{2,1,0:T(8,128)S(1)} %get-tuple-element.96), custom_call_target="InvertDiagBlocksLowerTriangular" | custom-call | tf_op jit(solution)/shard_map/jit(cholesky)/cholesky | solution.py:67
  573.6 11.7 %cholesky.257 = f32[128,128]{1,0:T(8,128)S(1)} custom-call(f32[128,128]{1,0:T(8,128)S(1)} %convolution_subtract_fusion.2), custom_call_target="Cholesky" | custom-call | tf_op jit(solution)/shard_map/jit(cholesky)/cholesky | solution.py:67
  588.0 4.3 while.8
  588.9 1.4 bitcast_dynamic-update-slice_fusion.8
  590.9 1.4 bitcast_dynamic-update-slice_fusion.8
  592.3 19.7 %custom-call.22 = f32[2,128,128]{1,2,0:T(8,128)S(1)} custom-call(f32[2,128,128]{2,1,0:T(8,128)S(1)} %get-tuple-element.28), custom_call_target="InvertDiagBlocksLowerTriangular" | custom-call | tf_op jit(solution)/shard_map/jit(_cho_solve)/triangular_solve | solution.py:69
  612.0 1.7 fusion.7
  616.7 1.4 maximum_bitcast_fusion.2
  618.1 1.3 maximum_bitcast_fusion.1
  619.4 1.4 maximum_bitcast_fusion
  621.5 39.2 %psum.31 = f32[3,2]{1,0:T(4,128)S(1)} all-reduce(f32[3,2]{1,0:T(4,128)S(1)} %pad_maximum_fusion), channel_id=1, replica_groups=mesh['row'=4,'col'=8] {'row','col'}, use_global_device_ids=true, to_apply=%region_22.25 | all-reduce | flops 6 | bytes 48 | tf_op jit(solution)/shard_map/psum | solution.py:76
  (135 shorter events, 26.1 us)
Async XLA Ops:
  8.0 1.1 copy-start.6
  8.0 137.1 %all-reduce.6.cloned.1.call-start = ((), (), s32[]{:S(2)}) async-start(), calls=%async_computation.3 | async-start | bytes 524288 | tf_op jit(solution)/shard_map/psum | solution.py:52
  9.2 8.3 %copy-start.4 = (s32[1,1,8,128,128]{4,3,2,1,0:T(8,128)S(1)}, s32[1,1,8,128,128]{4,3,2,1,0:T(8,128)}, u32[]{:S(2)}) copy-start(s32[1,1,8,128,128]{4,3,2,1,0:T(8,128)} %param.7) | copy-start | bytes 1572868
  10.2 7.3 %copy-start.7 = (s32[1,1,8]{2,1,0:T(1,128)S(1)}, s32[1,1,8]{2,1,0:T(1,128)}, u32[]{:S(2)}) copy-start(s32[1,1,8]{2,1,0:T(1,128)} %param.8) | copy-start | bytes 100
  10.2 196.7 %reduce-scatter.4.cloned.1.call-start = ((), (), s32[]{:S(2)}) async-start(), calls=%async_computation.4 | async-start | bytes 1179648 | tf_op jit(solution)/shard_map/reduce_scatter | solution.py:35
  21.6 325.0 %all-reduce.8.cloned.1.call-start = ((), (), s32[]{:S(2)}) async-start(), calls=%async_computation.5 | async-start | bytes 524288 | tf_op jit(solution)/shard_map/psum | solution.py:52
  44.1 0.7 copy-start.8
  146.1 1.0 copy-start
  219.4 189.6 %reduce-scatter.6.cloned.1.call-start = ((), (), s32[]{:S(2)}) async-start(), calls=%async_computation.6 | async-start | bytes 1179648 | tf_op jit(solution)/shard_map/reduce_scatter | solution.py:35
  220.0 329.5 %all-reduce.10.cloned.1.call-start = ((), (), s32[]{:S(2)}) async-start(), calls=%async_computation.7 | async-start | bytes 524288 | tf_op jit(solution)/shard_map/psum | solution.py:52
  347.6 1.0 copy-start.1
  422.2 189.8 %reduce-scatter.8.cloned.1.call-start = ((), (), s32[]{:S(2)}) async-start(), calls=%async_computation.8 | async-start | bytes 1179648 | tf_op jit(solution)/shard_map/reduce_scatter | solution.py:35
  550.5 1.0 copy-start.2
  587.9 24.1 %copy-start.5 = (f32[128,256]{0,1:T(8,128)S(1)}, f32[128,256]{0,1:T(8,128)}, u32[]{:S(2)}) copy-start(f32[128,256]{0,1:T(8,128)} %reduce-scatter.4.cloned.1.call-done) | copy-start | bytes 393220
  588.0 24.0 %copy-start.3 = (f32[128,256]{0,1:T(8,128)S(1)}, f32[128,256]{0,1:T(8,128)}, u32[]{:S(2)}) copy-start(f32[128,256]{0,1:T(8,128)} %reduce-scatter.6.cloned.1.call-done) | copy-start | bytes 393220
Sparse Core Ops, SparseCore 0:
  14.3 130.7 all-reduce.5
  219.5 127.0 all-reduce.7
  422.3 127.1 all-reduce.9
Sparse Core Ops, SparseCore 1:
  21.7 66.1 reduce-scatter.3
  223.3 63.7 reduce-scatter.5
  426.0 63.8 reduce-scatter.7
where the time goes:
time: 673 us; the launch traced here: 669 us
  waiting for transfers between devices  354 us (53%)
  other arithmetic  176 us (26%)
  blocking collectives  80.4 us (12%)
  local copies, waits for them, and re-layouts  25.8 us (4%)
  between operations  21.1 us (3%)
  matrix products  11.9 us (2%)
    psum x3, waiting for transfers between devices, local(): gram_total = lax.psum(own_gram, ('row', 'col'))  352 us
    another operation x20, other arithmetic, local(): triangle = jnp.linalg.cholesky(precond)  103 us
    another operation x7, other arithmetic, local(): jax.scipy.linalg.cho_solve((triangle, True), descent.T)  59.1 us
    psum x1, blocking collectives, local(): stacked = lax.psum(stacked, ('row', 'col'))  39.2 us
    unnamed x1, blocking collectives  22.3 us
    all_gather x3, blocking collectives, local(): lax.all_gather(packed, 'row', axis=0, tiled=True)  18.8 us
  transfers between devices with their start and end apart: 6, of which 3 were waited for; matrix products, arithmetic and copies ran while one was open for 27% of the time, Pallas kernels for 0%

commit v1 on v0

--- a/solution.py
+++ b/solution.py
@@ -49,7 +49,7 @@
         own_gram = lax.dot_general(
             packed, packed, (((0,), (0,)), ((), ())), preferred_element_type=jnp.float32
         )
-        gram_total = lax.psum(own_gram, ("row", "col"))
+        gram_total = lax.psum(lax.psum(own_gram, "col"), "row")
         gathered = lax.all_gather(packed, "row", axis=0, tiled=True).reshape(
             -1, piece_rows, columns
         )

time: 673 us -> 615 us (0.914)
  waiting for transfers between devices: 354 us -> 299 us
    psum x3 -> x6, waiting for transfers between devices: 352 us -> 278 us  [local(): gram_total = lax.psum(lax.psum(own_gram, 'col'), 'row')]
    reduce_scatter x3, waiting for transfers between devices: 0.08 us -> 19.2 us  [combine(): lax.psum_scatter(partial_value, 'col', scatter_dimension=0, tiled=True)]
  transfers between devices with their start and end apart: 6 -> 9, of which waited for: 3 -> 9; matrix products, arithmetic and copies ran while one was open for 27% -> 31% of each run, Pallas kernels for 0% -> 0%
where the time goes in v1:
time: 615 us; the launch traced here: 612 us
  waiting for transfers between devices  299 us (49%)
  other arithmetic  176 us (29%)
  blocking collectives  78.9 us (13%)
  local copies, waits for them, and re-layouts  25.8 us (4%)
  between operations  19.5 us (3%)
  matrix products  11.8 us (2%)
    psum x6, waiting for transfers between devices, local(): gram_total = lax.psum(lax.psum(own_gram, 'col'), 'row')  278 us
    another operation x20, other arithmetic, local(): triangle = jnp.linalg.cholesky(precond)  103 us
    another operation x7, other arithmetic, local(): jax.scipy.linalg.cho_solve((triangle, True), descent.T)  59.1 us
    psum x1, blocking collectives, local(): stacked = lax.psum(stacked, ('row', 'col'))  39.9 us
    unnamed x1, blocking collectives  20.1 us
    reduce_scatter x3, waiting for transfers between devices, combine(): lax.psum_scatter(partial_value, 'col', scatter_dimension=0, tiled=True)  19.2 us
    all_gather x3, blocking collectives, local(): lax.all_gather(packed, 'row', axis=0, tiled=True)  18.8 us
  transfers between devices with their start and end apart: 9, of which 9 were waited for; matrix products, arithmetic and copies ran while one was open for 31% of the time, Pallas kernels for 0%

profile of v1, /device:TPU:0, one launch (start us, length us, event | category | flops | bytes accessed | tf_op | source)
XLA Modules:
  0.0 611.6 jit_solution(6509748193314757352)
XLA Ops:
  7.2 1.0 copy.58
  9.4 7.2 %all_gather.9 = bf16[512,256]{0,1:T(8,128)(2,1)S(1)} all-gather(bf16[128,256]{0,1:T(8,128)(2,1)S(1)} %get-tuple-element.92), channel_id=1, replica_groups=mesh['row'=4,'col'=8] {'row'}, dimensions={0}, use_global_device_ids=true | all-gather | bytes 327680 | tf_op jit(solution)/shard_map/all_gather | solution.py:53
  17.9 67.2 %all-reduce.9.cloned.1.call-done = f32[256,256]{0,1:T(8,128)} async-done(((f32[256,256]{0,1:T(8,128)}), f32[256,256]{0,1:T(8,128)}) %all-reduce.9.cloned.1.call-update) | async-done | bytes 262160 | tf_op jit(solution)/shard_map/psum | solution.py:52
  85.2 1.2 fusion
  86.7 1.3 copy.53
  88.2 20.1 %all-reduce.1 = f32[1024]{0:T(1024)S(1)} all-reduce(f32[1024]{0:T(1024)S(1)} %convolution_bitcast_fusion), channel_id=2, replica_groups=mesh['row'=4,'col'=8] {'col'}, use_global_device_ids=true, to_apply=%region_7.9.clone | all-reduce | flops 1024 | bytes 8192
  110.3 8.6 %all-reduce.11.cloned.1.call-done = f32[256,256]{0,1:T(8,128)} async-done(((f32[256,256]{0,1:T(8,128)}), f32[256,256]{0,1:T(8,128)}) %all-reduce.11.cloned.1.call-update) | async-done | bytes 262160 | tf_op jit(solution)/shard_map/psum | solution.py:52
  118.9 1.0 select_add_fusion.2
  120.9 11.7 %cholesky.172 = f32[128,128]{1,0:T(8,128)S(1)} custom-call(f32[128,128]{1,0:T(8,128)S(1)} %cholesky.270), custom_call_target="Cholesky" | custom-call | tf_op jit(solution)/shard_map/jit(cholesky)/cholesky | solution.py:67
  132.7 9.8 %custom-call.17 = f32[1,128,128]{1,2,0:T(8,128)S(1)} custom-call(f32[1,128,128]{2,1,0:T(8,128)S(1)} %get-tuple-element.104), custom_call_target="InvertDiagBlocksLowerTriangular" | custom-call | tf_op jit(solution)/shard_map/jit(cholesky)/cholesky | solution.py:67
  143.0 11.7 %cholesky.189 = f32[128,128]{1,0:T(8,128)S(1)} custom-call(f32[128,128]{1,0:T(8,128)S(1)} %convolution_subtract_fusion.8), custom_call_target="Cholesky" | custom-call | tf_op jit(solution)/shard_map/jit(cholesky)/cholesky | solution.py:67
  156.8 4.2 while.6
  157.6 1.4 bitcast_dynamic-update-slice_fusion.6
  159.6 1.4 bitcast_dynamic-update-slice_fusion.6
  161.0 19.7 %custom-call.18 = f32[2,128,128]{1,2,0:T(8,128)S(1)} custom-call(f32[2,128,128]{2,1,0:T(8,128)S(1)} %get-tuple-element.26), custom_call_target="InvertDiagBlocksLowerTriangular" | custom-call | tf_op jit(solution)/shard_map/jit(_cho_solve)/triangular_solve | solution.py:69
  180.7 6.9 %reduce-scatter.4.cloned.1.call-done = f32[128,256]{0,1:T(8,128)} async-done(((f32[1024,256]{0,1:T(8,128)}), f32[128,256]{0,1:T(8,128)}) %reduce-scatter.4.cloned.1.call-update) | async-done | bytes 131088 | tf_op jit(solution)/shard_map/reduce_scatter | solution.py:35
  190.1 5.8 all_gather.10
  198.9 1.2 copy.91
  200.1 68.2 %all-reduce.13.cloned.1.call-done = f32[256,256]{0,1:T(8,128)} async-done(((f32[256,256]{0,1:T(8,128)}), f32[256,256]{0,1:T(8,128)}) %all-reduce.13.cloned.1.call-update) | async-done | bytes 262160 | tf_op jit(solution)/shard_map/psum | solution.py:52
  269.0 33.0 %all-reduce.15.cloned.1.call-done = f32[256,256]{0,1:T(8,128)} async-done(((f32[256,256]{0,1:T(8,128)}), f32[256,256]{0,1:T(8,128)}) %all-reduce.15.cloned.1.call-update) | async-done | bytes 262160 | tf_op jit(solution)/shard_map/psum | solution.py:52
  302.0 1.0 select_add_fusion.1
  304.0 11.7 %cholesky.206 = f32[128,128]{1,0:T(8,128)S(1)} custom-call(f32[128,128]{1,0:T(8,128)S(1)} %cholesky.273), custom_call_target="Cholesky" | custom-call | tf_op jit(solution)/shard_map/jit(cholesky)/cholesky | solution.py:67
  315.8 9.8 %custom-call.19 = f32[1,128,128]{1,2,0:T(8,128)S(1)} custom-call(f32[1,128,128]{2,1,0:T(8,128)S(1)} %get-tuple-element.100), custom_call_target="InvertDiagBlocksLowerTriangular" | custom-call | tf_op jit(solution)/shard_map/jit(cholesky)/cholesky | solution.py:67
  326.1 11.7 %cholesky.223 = f32[128,128]{1,0:T(8,128)S(1)} custom-call(f32[128,128]{1,0:T(8,128)S(1)} %convolution_subtract_fusion.5), custom_call_target="Cholesky" | custom-call | tf_op jit(solution)/shard_map/jit(cholesky)/cholesky | solution.py:67
  340.5 4.2 while.7
  341.3 1.4 bitcast_dynamic-update-slice_fusion.7
  343.3 1.4 bitcast_dynamic-update-slice_fusion.7
  344.7 19.7 %custom-call.20 = f32[2,128,128]{1,2,0:T(8,128)S(1)} custom-call(f32[2,128,128]{2,1,0:T(8,128)S(1)} %get-tuple-element.27), custom_call_target="InvertDiagBlocksLowerTriangular" | custom-call | tf_op jit(solution)/shard_map/jit(_cho_solve)/triangular_solve | solution.py:69
  364.4 6.2 %reduce-scatter.6.cloned.1.call-done = f32[128,256]{0,1:T(8,128)} async-done(((f32[1024,256]{0,1:T(8,128)}), f32[128,256]{0,1:T(8,128)}) %reduce-scatter.6.cloned.1.call-update) | async-done | bytes 131088 | tf_op jit(solution)/shard_map/reduce_scatter | solution.py:35
  370.6 1.6 subtract_bitcast_fusion.1
  374.6 5.8 all_gather.11
  382.5 1.2 copy.90
  383.7 68.3 %all-reduce.17.cloned.1.call-done = f32[256,256]{0,1:T(8,128)} async-done(((f32[256,256]{0,1:T(8,128)}), f32[256,256]{0,1:T(8,128)}) %all-reduce.17.cloned.1.call-update) | async-done | bytes 262160 | tf_op jit(solution)/shard_map/psum | solution.py:52
  452.8 33.1 %all-reduce.19.cloned.1.call-done = f32[256,256]{0,1:T(8,128)} async-done(((f32[256,256]{0,1:T(8,128)}), f32[256,256]{0,1:T(8,128)}) %all-reduce.19.cloned.1.call-update) | async-done | bytes 262160 | tf_op jit(solution)/shard_map/psum | solution.py:52
  485.9 1.0 select_add_fusion
  487.9 11.7 %cholesky.240 = f32[128,128]{1,0:T(8,128)S(1)} custom-call(f32[128,128]{1,0:T(8,128)S(1)} %cholesky.276), custom_call_target="Cholesky" | custom-call | tf_op jit(solution)/shard_map/jit(cholesky)/cholesky | solution.py:67
  499.7 9.8 %custom-call.21 = f32[1,128,128]{1,2,0:T(8,128)S(1)} custom-call(f32[1,128,128]{2,1,0:T(8,128)S(1)} %get-tuple-element.96), custom_call_target="InvertDiagBlocksLowerTriangular" | custom-call | tf_op jit(solution)/shard_map/jit(cholesky)/cholesky | solution.py:67
  510.0 11.7 %cholesky.257 = f32[128,128]{1,0:T(8,128)S(1)} custom-call(f32[128,128]{1,0:T(8,128)S(1)} %convolution_subtract_fusion.2), custom_call_target="Cholesky" | custom-call | tf_op jit(solution)/shard_map/jit(cholesky)/cholesky | solution.py:67
  524.4 4.3 while.8
  525.2 1.4 bitcast_dynamic-update-slice_fusion.8
  527.2 1.4 bitcast_dynamic-update-slice_fusion.8
  528.6 19.7 %custom-call.22 = f32[2,128,128]{1,2,0:T(8,128)S(1)} custom-call(f32[2,128,128]{2,1,0:T(8,128)S(1)} %get-tuple-element.28), custom_call_target="InvertDiagBlocksLowerTriangular" | custom-call | tf_op jit(solution)/shard_map/jit(_cho_solve)/triangular_solve | solution.py:69
  548.3 6.2 %reduce-scatter.8.cloned.1.call-done = f32[128,256]{0,1:T(8,128)} async-done(((f32[1024,256]{0,1:T(8,128)}), f32[128,256]{0,1:T(8,128)}) %reduce-scatter.8.cloned.1.call-update) | async-done | bytes 131088 | tf_op jit(solution)/shard_map/reduce_scatter | solution.py:35
  554.5 1.7 fusion.7
  559.2 1.4 maximum_bitcast_fusion.2
  560.6 1.3 maximum_bitcast_fusion.1
  561.9 1.4 maximum_bitcast_fusion
  564.0 39.9 %psum.55 = f32[3,2]{1,0:T(4,128)S(1)} all-reduce(f32[3,2]{1,0:T(4,128)S(1)} %pad_maximum_fusion), channel_id=1, replica_groups=mesh['row'=4,'col'=8] {'row','col'}, use_global_device_ids=true, to_apply=%region_25.28 | all-reduce | flops 6 | bytes 48 | tf_op jit(solution)/shard_map/psum | solution.py:76
  (144 shorter events, 31.6 us)
Async XLA Ops:
  7.2 1.1 copy-start.6
  7.2 77.9 %all-reduce.9.cloned.1.call-start = ((), (), s32[]{:S(2)}) async-start(), calls=%async_computation.3 | async-start | bytes 524288 | tf_op jit(solution)/shard_map/psum | solution.py:52
  8.4 8.2 %copy-start.4 = (s32[1,1,8,128,128]{4,3,2,1,0:T(8,128)S(1)}, s32[1,1,8,128,128]{4,3,2,1,0:T(8,128)}, u32[]{:S(2)}) copy-start(s32[1,1,8,128,128]{4,3,2,1,0:T(8,128)} %param.7) | copy-start | bytes 1572868
  9.3 7.3 %copy-start.7 = (s32[1,1,8]{2,1,0:T(1,128)S(1)}, s32[1,1,8]{2,1,0:T(1,128)}, u32[]{:S(2)}) copy-start(s32[1,1,8]{2,1,0:T(1,128)} %param.8) | copy-start | bytes 100
  9.3 109.6 %all-reduce.11.cloned.1.call-start = ((), (), s32[]{:S(2)}) async-start(), calls=%async_computation.4 | async-start | bytes 524288 | tf_op jit(solution)/shard_map/psum | solution.py:52
  85.1 102.5 %reduce-scatter.4.cloned.1.call-start = ((), (), s32[]{:S(2)}) async-start(), calls=%async_computation.5 | async-start | bytes 1179648 | tf_op jit(solution)/shard_map/reduce_scatter | solution.py:35
  88.0 180.3 %all-reduce.13.cloned.1.call-start = ((), (), s32[]{:S(2)}) async-start(), calls=%async_computation.6 | async-start | bytes 524288 | tf_op jit(solution)/shard_map/psum | solution.py:52
  108.4 0.7 copy-start.8
  119.9 1.0 copy-start
  198.2 103.8 %all-reduce.15.cloned.1.call-start = ((), (), s32[]{:S(2)}) async-start(), calls=%async_computation.7 | async-start | bytes 524288 | tf_op jit(solution)/shard_map/psum | solution.py:52
  268.4 102.2 %reduce-scatter.6.cloned.1.call-start = ((), (), s32[]{:S(2)}) async-start(), calls=%async_computation.8 | async-start | bytes 1179648 | tf_op jit(solution)/shard_map/reduce_scatter | solution.py:35
  269.0 183.1 %all-reduce.17.cloned.1.call-start = ((), (), s32[]{:S(2)}) async-start(), calls=%async_computation.9 | async-start | bytes 524288 | tf_op jit(solution)/shard_map/psum | solution.py:52
  303.0 1.0 copy-start.1
  381.9 104.0 %all-reduce.19.cloned.1.call-start = ((), (), s32[]{:S(2)}) async-start(), calls=%async_computation.10 | async-start | bytes 524288 | tf_op jit(solution)/shard_map/psum | solution.py:52
  452.1 102.4 %reduce-scatter.8.cloned.1.call-start = ((), (), s32[]{:S(2)}) async-start(), calls=%async_computation.11 | async-start | bytes 1179648 | tf_op jit(solution)/shard_map/reduce_scatter | solution.py:35
  486.9 1.0 copy-start.2
  524.3 30.2 %copy-start.5 = (f32[128,256]{0,1:T(8,128)S(1)}, f32[128,256]{0,1:T(8,128)}, u32[]{:S(2)}) copy-start(f32[128,256]{0,1:T(8,128)} %reduce-scatter.4.cloned.1.call-done) | copy-start | bytes 393220
  524.3 30.1 %copy-start.3 = (f32[128,256]{0,1:T(8,128)S(1)}, f32[128,256]{0,1:T(8,128)}, u32[]{:S(2)}) copy-start(f32[128,256]{0,1:T(8,128)} %reduce-scatter.6.cloned.1.call-done) | copy-start | bytes 393220
Sparse Core Ops, SparseCore 0:
  11.3 73.7 all-reduce.8
  87.4 31.4 all-reduce.10
  122.3 65.1 reduce-scatter.3
  198.4 69.9 all-reduce.12
  270.5 31.4 all-reduce.14
  305.3 65.2 reduce-scatter.5
  382.0 70.0 all-reduce.16
  454.4 31.4 all-reduce.18
  489.3 65.1 reduce-scatter.7
